TPU v7x, 128 devices: a whole 4x4x4 slice. The times are simulated.
128 devices in a mesh: dom: 32 (over z, y, core), col: 2 (over x_hi), batch: 2 (over x_lo).
Axes of the slice: x: 4 (x_hi: 2, x_lo: 2; x = x_hi * 2 + x_lo), y: 4, z: 4, core: 2. Of those that a mesh axis runs over, the one named last changes fastest.
Arguments:
- features: bfloat16 [65536, 128], P('dom', 'col'), may hold values from -6 to 6
- self_weight1: bfloat16 [128, 256], P('col', 'batch'), may hold values from -0.5 to 0.5
- neigh_weight1: bfloat16 [128, 256], P('col', 'batch'), may hold values from -2 to 2
- need_first: int32 [64, 64], P(('dom', 'batch')), may hold values from 0 to 511, as said below
- count_first: int32 [64], P(('dom', 'batch')), may hold values from 0 to 64
- adjacency_first: int32 [65536, 512], P(('dom', 'batch')), may hold values from 0 to 16384, as said below
- self_weight2: bfloat16 [256, 172], P('col', 'batch'), may hold values from -0.375 to 0.375
- neigh_weight2: bfloat16 [256, 172], P('col', 'batch'), may hold values from -0.375 to 0.375
- need_second: int32 [64, 64], P(('dom', 'batch')), may hold values from 0 to 511, as said below
- count_second: int32 [64], P(('dom', 'batch')), may hold values from 0 to 64
- adjacency_second: int32 [65536, 512], P(('dom', 'batch')), may hold values from 0 to 16384, as said below
- seed_rows: int32 [65536], P(('dom', 'batch')), may hold values from 0 to 2047
Outputs:
- logits: float32 [65536, 172], P(('dom', 'batch'))
Inputs may be any that keep to these rules, and one draw needn't show every extreme that they name: `need_first`: each row lists 64 different node blocks in increasing order; block g holds nodes 128 * g to 128 * g + 127 and lies in partition g // 16. At most 4 entries of one row lie in one partition, and exactly 4 lie in some partition in every row. `need_second`: each row lists 64 different frontier blocks in increasing order; block g holds frontier rows 128 * g to 128 * g + 127 and lies in partition g // 16. At most 4 entries of one row lie in one partition, and exactly 4 lie in some partition in every row. `adjacency_first`: bit i of word k of a row is the adjacency entry of column 16 k + i; at most one bit of a word is set, and bit 15 never. `adjacency_second`: bit i of word k of a row is the adjacency entry of column 16 k + i; at most one bit of a word is set, and bit 15 never.
All inputs are finite; a program needn't handle non-finite values.
Results may differ from a plain program's by a relative error of at most 0.0036.
Values may be sent and summed in bfloat16 or wider, within the bound.
A program may use at most 128 MiB of HBM per device.

v0:
```python
import math

import jax
import jax.numpy as jnp
from jax import lax
from jax.sharding import PartitionSpec as P

BLK = 128


def in_blocks(shard, dim, devices):
    shape = shard.shape
    blocks = shard.reshape(*shape[:dim], devices, shape[dim] // devices, *shape[dim + 1 :])
    return jnp.moveaxis(blocks, dim, 0)


def sent_and_summed(shard, axis, dim):
    devices = lax.axis_size(axis)
    blocks = lax.all_to_all(in_blocks(shard, dim, devices), axis, 0, 0, tiled=True)
    return jnp.sum(blocks, axis=0)


def from_everyone(shard, axis):
    copies = jnp.broadcast_to(shard, (lax.axis_size(axis), *shard.shape))
    return lax.all_to_all(copies, axis, split_axis=0, concat_axis=0, tiled=True)


def of_everyone(shard, axis):
    return from_everyone(shard, axis).sum(axis=0)


def unpack_rows(packed_rows, valid_cols):
    shifts = jnp.arange(16, dtype=jnp.int32)
    bit_table = jnp.right_shift(packed_rows[:, :, None], shifts[None, None, :]) & 1
    bit_table = bit_table.reshape(packed_rows.shape[0], packed_rows.shape[1] * 16)
    column = jnp.arange(bit_table.shape[1], dtype=jnp.int32)
    return jnp.where(column[None, :] < valid_cols, bit_table, 0)


def mean_rows(packed, valid_cols, needed):
    total_rows = packed.shape[0]
    row_block = math.gcd(total_rows, 256)
    grouped = packed.reshape(total_rows // row_block, row_block, packed.shape[1])

    def one_block(row_piece):
        dense_rows = unpack_rows(row_piece, valid_cols)
        degree = jnp.sum(dense_rows, axis=1).astype(jnp.float32)
        summed = jnp.dot(
            dense_rows.astype(jnp.bfloat16), needed, preferred_element_type=jnp.float32
        )
        return (summed / jnp.maximum(degree, 1.0)[:, None]).astype(jnp.bfloat16)

    return lax.map(one_block, grouped).reshape(total_rows, needed.shape[1])


def pick_blocks(holding, wanted, arriving):
    inside = (wanted >= 0) & (wanted < arriving.shape[0])
    taken_rows = jnp.take(arriving, jnp.clip(wanted, 0, arriving.shape[0] - 1), axis=0)
    return jnp.where(inside[:, None], taken_rows, holding)


def per_device(
    features,
    self_weight1,
    neigh_weight1,
    need_first,
    count_first,
    adjacency_first,
    self_weight2,
    neigh_weight2,
    need_second,
    count_second,
    adjacency_second,
    seed_rows,
):
    batch_at = lax.axis_index("batch")
    rows_first = adjacency_first.shape[0]
    node_blocks = features.reshape(features.shape[0] // BLK, BLK * features.shape[1])
    wanted_first = need_first[0]
    empty_first = jnp.zeros((wanted_first.shape[0], node_blocks.shape[1]), jnp.bfloat16)
    fetched_first = pick_blocks(
        empty_first, wanted_first, lax.all_gather(node_blocks, "dom", axis=0, tiled=True)
    )
    needed_first = fetched_first.reshape(-1, features.shape[1])
    near_first = mean_rows(adjacency_first, count_first[0] * BLK, needed_first)
    self_first = lax.dynamic_slice_in_dim(features, batch_at * rows_first, rows_first, 0)
    weight_self, weight_near = (
        lax.all_gather(self_weight1, "batch", axis=1, tiled=True),
        lax.all_gather(neigh_weight1, "batch", axis=1, tiled=True),
    )
    partial_first = jnp.dot(self_first, weight_self, preferred_element_type=jnp.float32) + jnp.dot(
        near_first, weight_near, preferred_element_type=jnp.float32
    )
    summed_first = sent_and_summed(partial_first, "col", 1)
    hidden_first = jnp.maximum(summed_first, 0.0).astype(jnp.bfloat16)
    frontier = lax.all_gather(hidden_first, "batch", axis=0, tiled=True)
    front_blocks = frontier.reshape(frontier.shape[0] // BLK, BLK * frontier.shape[1])
    wanted_second = need_second[0]
    empty_second = jnp.zeros((wanted_second.shape[0], front_blocks.shape[1]), jnp.bfloat16)
    fetched_second = pick_blocks(
        empty_second, wanted_second, lax.all_gather(front_blocks, "dom", axis=0, tiled=True)
    )
    needed_second = fetched_second.reshape(-1, frontier.shape[1])
    near_second = mean_rows(adjacency_second, count_second[0] * BLK, needed_second)
    own_second = jnp.take(frontier, seed_rows, axis=0)
    weight_own, weight_far = (
        lax.all_gather(self_weight2, "batch", axis=1, tiled=True),
        lax.all_gather(neigh_weight2, "batch", axis=1, tiled=True),
    )
    partial_second = jnp.dot(own_second, weight_own, preferred_element_type=jnp.float32) + jnp.dot(
        near_second, weight_far, preferred_element_type=jnp.float32
    )
    return of_everyone(partial_second, "col")


def solution(mesh):
    placed = (
        P("dom", "col"),
        P("col", "batch"),
        P("col", "batch"),
        P(("dom", "batch"), None),
        P(("dom", "batch")),
        P(("dom", "batch"), None),
        P("col", "batch"),
        P("col", "batch"),
        P(("dom", "batch"), None),
        P(("dom", "batch")),
        P(("dom", "batch"), None),
        P(("dom", "batch")),
    )
    return jax.shard_map(
        per_device, mesh=mesh, in_specs=placed, out_specs=P(("dom", "batch"), None), check_vma=False
    )
```

profile of v0, /device:TPU:0, one launch (start us, length us, event | category | flops | bytes accessed | tf_op | source)
XLA Modules:
  0.0 310.1 jit_solution(4355814135532355377)
XLA Ops:
  9.7 4.6 %all_gather.21 = bf16[64,256]{1,0:T(8,128)(2,1)S(1)} all-gather(bf16[64,128]{1,0:T(8,128)(2,1)} %param.17), channel_id=1, replica_groups=mesh['dom'=32,'col'=2,'batch'=2] {'batch'}, dimensions={1}, use_global_device_ids=true | all-gather | bytes 49152 | tf_op jit(solution)/shard_map/all_gather | solution.py:88
  14.3 4.6 %all_gather.23 = bf16[64,256]{1,0:T(8,128)(2,1)S(1)} all-gather(bf16[64,128]{1,0:T(8,128)(2,1)} %param.18), channel_id=1, replica_groups=mesh['dom'=32,'col'=2,'batch'=2] {'batch'}, dimensions={1}, use_global_device_ids=true | all-gather | bytes 49152 | tf_op jit(solution)/shard_map/all_gather | solution.py:89
  23.4 41.6 %all-gather.5.cloned.1.call-done = bf16[512,8192]{1,0:T(8,128)(2,1)} async-done(((bf16[16,8192]{1,0:T(8,128)(2,1)}), bf16[512,8192]{1,0:T(8,128)(2,1)}) %all-gather.5.cloned.1.call-update) | async-done | bytes 8388624 | tf_op jit(solution)/shard_map/all_gather | solution.py:82
  65.0 6.6 %gather_fusion = bf16[64,8192]{1,0:T(8,128)(2,1)S(1)} fusion(bf16[512,8192]{1,0:T(8,128)(2,1)} %all-gather.5.cloned.1.call-done, s32[1024]{0:T(1024)S(1)} %pad_clamp_fusion.1), kind=kCustom, calls=%fused_computation | custom fusion | bytes 2097408 | tf_op jit(solution)/shard_map/jit(_take)/gather | solution.py:58
  71.6 3.3 %gather.17 = bf16[8192,64]{1,0:T(8,128)(2,1)} reshape(bf16[64,8192]{1,0:T(8,128)(2,1)S(1)} %gather_fusion) | data formatting | bytes 2097152 | tf_op jit(solution)/shard_map/jit(_take)/gather | solution.py:58
  74.9 7.0 %select_select_fusion.1 = bf16[8192,64]{1,0:T(8,128)(2,1)S(1)} fusion(bf16[8192,64]{1,0:T(8,128)(2,1)} %gather.17, pred[8192]{0:T(1024)(128)(4,1)S(1)} %get-tuple-element.101, pred[8192]{0:T(1024)(128)(4,1)S(1)} %get-tuple-element.102), kind=kLoop, calls=%fused_computation.30 | loop fusion | flops 1048576 | bytes 2113536 | tf_op jit(solution)/shard_map/jit(_where)/select_n | solution.py:59
  81.9 36.0 %while.20 = (s32[]{:T(128)}, bf16[4,256,64]{1,2,0:T(8,128)(2,1)S(1)}, s32[]{:T(128)}, s32[4,256,512]{2,1,0:T(8,128)}, bf16[8192,64]{1,0:T(8,128)(2,1)S(1)}, /*index=5*/s32[]{:T(128)}) while((s32[]{:T(128)}, bf16[4,256,64]{1,2,0:T(8,128)(2,1)S(1)}, s32[]{:T(128)}, s32[4,256,512]{2,1,0:T(8,128)}, bf16[8192,64]{1,0:T(8,128)(2,1)S(1)}, ...), condition=%wide.region_2.3_spmd, body=%wide.region_0.2_spmd.sunk | while | flops 285278464 | bytes 13832277 | solution.py:53
  83.4 2.8 fusion.43
  86.2 3.6 %select_reduce_fusion.4 = s32[256]{0:T(256)S(1)} fusion(s32[256,512]{0,1:T(8,128)S(1)} %bitcast.97, pred[512,16]{1,0:T(8,128)(4,1)S(1)} %add_compare_fusion.4), kind=kLoop, calls=%fused_computation.7.clone.1 | loop fusion | flops 8388352 | bytes 533504 | tf_op jit(solution)/shard_map/while/body/eval_jaxpr/reduce_sum | solution.py:47
  92.4 2.8 fusion.43
  95.2 3.6 %select_reduce_fusion.4 = s32[256]{0:T(256)S(1)} fusion(s32[256,512]{0,1:T(8,128)S(1)} %bitcast.97, pred[512,16]{1,0:T(8,128)(4,1)S(1)} %add_compare_fusion.4), kind=kLoop, calls=%fused_computation.7.clone.1 | loop fusion | flops 8388352 | bytes 533504 | tf_op jit(solution)/shard_map/while/body/eval_jaxpr/reduce_sum | solution.py:47
  101.4 2.8 fusion.43
  104.2 3.6 %select_reduce_fusion.4 = s32[256]{0:T(256)S(1)} fusion(s32[256,512]{0,1:T(8,128)S(1)} %bitcast.97, pred[512,16]{1,0:T(8,128)(4,1)S(1)} %add_compare_fusion.4), kind=kLoop, calls=%fused_computation.7.clone.1 | loop fusion | flops 8388352 | bytes 533504 | tf_op jit(solution)/shard_map/while/body/eval_jaxpr/reduce_sum | solution.py:47
  110.4 2.8 fusion.43
  113.2 3.6 %select_reduce_fusion.4 = s32[256]{0:T(256)S(1)} fusion(s32[256,512]{0,1:T(8,128)S(1)} %bitcast.97, pred[512,16]{1,0:T(8,128)(4,1)S(1)} %add_compare_fusion.4), kind=kLoop, calls=%fused_computation.7.clone.1 | loop fusion | flops 8388352 | bytes 533504 | tf_op jit(solution)/shard_map/while/body/eval_jaxpr/reduce_sum | solution.py:47
  119.5 19.6 %all_to_all.10 = f32[2,1024,128]{1,2,0:T(8,128)S(1)} all-to-all(f32[2,1024,128]{1,2,0:T(8,128)S(1)} %bitcast.100), channel_id=1, replica_groups=mesh['dom'=32,'col'=2,'batch'=2] {'col'}, dimensions={0} | all-to-all | bytes 2097152 | tf_op jit(solution)/shard_map/all_to_all | solution.py:19
  139.4 8.0 %all_gather.24 = bf16[2048,128]{1,0:T(8,128)(2,1)S(1)} all-gather(bf16[1024,128]{1,0:T(8,128)(2,1)S(1)} %maximum_convert_fusion), channel_id=1, replica_groups=mesh['dom'=32,'col'=2,'batch'=2] {'batch'}, dimensions={0}, use_global_device_ids=true | all-gather | bytes 786432 | tf_op jit(solution)/shard_map/all_gather | solution.py:96
  149.1 4.5 %all-gather = bf16[2,86,128]{2,1,0:T(8,128)(2,1)S(1)} all-gather(bf16[1,86,128]{2,1,0:T(8,128)(2,1)S(1)} %bitcast.106), channel_id=1, replica_groups=mesh['dom'=32,'col'=2,'batch'=2] {'batch'}, dimensions={0}, use_global_device_ids=true | all-gather | bytes 66048 | tf_op jit(solution)/shard_map/all_gather | solution.py:107
  153.6 4.7 %all-gather.1 = bf16[2,86,128]{2,1,0:T(8,128)(2,1)S(1)} all-gather(bf16[1,86,128]{2,1,0:T(8,128)(2,1)S(1)} %bitcast.107), channel_id=1, replica_groups=mesh['dom'=32,'col'=2,'batch'=2] {'batch'}, dimensions={0}, use_global_device_ids=true | all-gather | bytes 66048 | tf_op jit(solution)/shard_map/all_gather | solution.py:108
  158.5 3.2 %gather_fusion.1 = bf16[1024,128]{1,0:T(8,128)(2,1)S(1)} fusion(bf16[2048,128]{1,0:T(8,128)(2,1)S(1)} %all_gather.24, s32[1024]{0:T(1024)S(1)} %fusion.18), kind=kCustom, calls=%fused_computation.1 | custom fusion | bytes 528384 | tf_op jit(solution)/shard_map/jit(_take)/gather | solution.py:105
  162.1 56.3 %all-gather.7.cloned.1.call-done = bf16[512,16384]{1,0:T(8,128)(2,1)} async-done(((bf16[16,16384]{1,0:T(8,128)(2,1)}), bf16[512,16384]{1,0:T(8,128)(2,1)}) %all-gather.7.cloned.1.call-update) | async-done | bytes 16777232 | tf_op jit(solution)/shard_map/all_gather | solution.py:101
  218.3 12.9 %gather_fusion.2 = bf16[64,16384]{1,0:T(8,128)(2,1)} fusion(bf16[512,16384]{1,0:T(8,128)(2,1)} %all-gather.7.cloned.1.call-done, s32[1024]{0:T(1024)S(1)} %pad_clamp_fusion), kind=kCustom, calls=%fused_computation.2 | custom fusion | bytes 4194560 | tf_op jit(solution)/shard_map/jit(_take)/gather | solution.py:58
  231.3 2.9 gather.20
  234.2 6.7 %select_select_fusion = bf16[8192,128]{1,0:T(8,128)(2,1)} fusion(bf16[8192,128]{1,0:T(8,128)(2,1)S(1)} %gather.20, pred[8192]{0:T(1024)(128)(4,1)S(1)} %get-tuple-element.103, pred[8192]{0:T(1024)(128)(4,1)S(1)} %get-tuple-element.104), kind=kLoop, calls=%fused_computation.29 | loop fusion | flops 2097152 | bytes 4210688 | tf_op jit(solution)/shard_map/jit(_where)/select_n | solution.py:59
  240.9 37.2 %while.21 = (s32[]{:T(128)}, bf16[4,256,128]{2,1,0:T(8,128)(2,1)S(1)}, s32[]{:T(128)}, s32[4,256,512]{2,1,0:T(8,128)}, bf16[8192,128]{1,0:T(8,128)(2,1)}, /*index=5*/s32[]{:T(128)}) while((s32[]{:T(128)}, bf16[4,256,128]{2,1,0:T(8,128)(2,1)S(1)}, s32[]{:T(128)}, s32[4,256,512]{2,1,0:T(8,128)}, bf16[8192,128]{1,0:T(8,128)(2,1)}, ...), condition=%wide.region_6.7_spmd, body=%wide.region_4.6_spmd.sunk | while | flops 553746688 | bytes 22253680 | solution.py:53
  242.3 2.8 fusion.47
  245.2 3.6 %select_reduce_fusion.5 = s32[256]{0:T(256)S(1)} fusion(s32[256,512]{0,1:T(8,128)S(1)} %bitcast.99, pred[512,16]{1,0:T(8,128)(4,1)S(1)} %add_compare_fusion.5), kind=kLoop, calls=%fused_computation.20.clone.1 | loop fusion | flops 8388352 | bytes 533504 | tf_op jit(solution)/shard_map/while/body/eval_jaxpr/reduce_sum | solution.py:47
  254.5 3.6 %select_reduce_fusion.5 = s32[256]{0:T(256)S(1)} fusion(s32[256,512]{0,1:T(8,128)S(1)} %bitcast.99, pred[512,16]{1,0:T(8,128)(4,1)S(1)} %add_compare_fusion.5), kind=kLoop, calls=%fused_computation.20.clone.1 | loop fusion | flops 8388352 | bytes 533504 | tf_op jit(solution)/shard_map/while/body/eval_jaxpr/reduce_sum | solution.py:47
  261.0 2.8 fusion.47
  263.8 3.6 %select_reduce_fusion.5 = s32[256]{0:T(256)S(1)} fusion(s32[256,512]{0,1:T(8,128)S(1)} %bitcast.99, pred[512,16]{1,0:T(8,128)(4,1)S(1)} %add_compare_fusion.5), kind=kLoop, calls=%fused_computation.20.clone.1 | loop fusion | flops 8388352 | bytes 533504 | tf_op jit(solution)/shard_map/while/body/eval_jaxpr/reduce_sum | solution.py:47
  273.1 3.6 %select_reduce_fusion.5 = s32[256]{0:T(256)S(1)} fusion(s32[256,512]{0,1:T(8,128)S(1)} %bitcast.99, pred[512,16]{1,0:T(8,128)(4,1)S(1)} %add_compare_fusion.5), kind=kLoop, calls=%fused_computation.20.clone.1 | loop fusion | flops 8388352 | bytes 533504 | tf_op jit(solution)/shard_map/while/body/eval_jaxpr/reduce_sum | solution.py:47
  278.5 23.8 %all_to_all.11 = f32[2,1024,172]{1,2,0:T(8,128)S(1)} all-to-all(f32[2,1024,172]{1,2,0:T(8,128)S(1)} %broadcast_in_dim.146), channel_id=1, replica_groups=mesh['dom'=32,'col'=2,'batch'=2] {'col'}, dimensions={0} | all-to-all | bytes 2818048 | tf_op jit(solution)/shard_map/all_to_all | solution.py:25
  (115 shorter events, 38.8 us)
Async XLA Ops:
  6.5 58.5 %all-gather.5.cloned.1.call-start = ((), (), s32[]{:S(2)}) async-start(), calls=%async_computation.2 | async-start | bytes 8650752 | tf_op jit(solution)/shard_map/all_gather | solution.py:82
  9.0 209.4 %all-gather.7.cloned.1.call-start = ((), (), s32[]{:S(2)}) async-start(), calls=%async_computation.3 | async-start | bytes 17301504 | tf_op jit(solution)/shard_map/all_gather | solution.py:101
  117.9 31.2 %copy-start.1 = (bf16[128,86]{0,1:T(8,128)(2,1)S(1)}, bf16[128,86]{0,1:T(8,128)(2,1)}, u32[]{:S(2)}) copy-start(bf16[128,86]{0,1:T(8,128)(2,1)} %param.22) | copy-start | bytes 66052
  117.9 35.7 %copy-start.2 = (bf16[128,86]{0,1:T(8,128)(2,1)S(1)}, bf16[128,86]{0,1:T(8,128)(2,1)}, u32[]{:S(2)}) copy-start(bf16[128,86]{0,1:T(8,128)(2,1)} %param.23) | copy-start | bytes 66052
  117.9 40.3 %copy-start.4 = (s32[1,64]{1,0:T(1,128)S(1)}, s32[1,64]{1,0:T(1,128)}, u32[]{:S(2)}) copy-start(s32[1,64]{1,0:T(1,128)} %param.24) | copy-start | bytes 772
  117.9 40.4 %copy-start.3 = (s32[1024]{0:T(1024)S(1)}, s32[1024]{0:T(1024)}, u32[]{:S(2)}) copy-start(s32[1024]{0:T(1024)} %param.27) | copy-start | bytes 12292
  242.3 6.5 %copy-start = (bf16[8192,128]{1,0:T(8,128)(2,1)S(1)}, bf16[8192,128]{1,0:T(8,128)(2,1)}, u32[]{:S(2)}) copy-start(bf16[8192,128]{1,0:T(8,128)(2,1)} %get-tuple-element.201) | copy-start | bytes 6291460 | tf_op jit(solution)/shard_map/while
  251.6 6.5 %copy-start = (bf16[8192,128]{1,0:T(8,128)(2,1)S(1)}, bf16[8192,128]{1,0:T(8,128)(2,1)}, u32[]{:S(2)}) copy-start(bf16[8192,128]{1,0:T(8,128)(2,1)} %get-tuple-element.201) | copy-start | bytes 6291460 | tf_op jit(solution)/shard_map/while
  260.9 6.5 %copy-start = (bf16[8192,128]{1,0:T(8,128)(2,1)S(1)}, bf16[8192,128]{1,0:T(8,128)(2,1)}, u32[]{:S(2)}) copy-start(bf16[8192,128]{1,0:T(8,128)(2,1)} %get-tuple-element.201) | copy-start | bytes 6291460 | tf_op jit(solution)/shard_map/while
  270.3 6.5 %copy-start = (bf16[8192,128]{1,0:T(8,128)(2,1)S(1)}, bf16[8192,128]{1,0:T(8,128)(2,1)}, u32[]{:S(2)}) copy-start(bf16[8192,128]{1,0:T(8,128)(2,1)} %get-tuple-element.201) | copy-start | bytes 6291460 | tf_op jit(solution)/shard_map/while
Sparse Core Ops, SparseCore 0:
  9.6 55.3 all-gather.4
  148.5 69.7 all-gather.6
where the time goes:
time: 311 us; the launch traced here: 310 us
  waiting for transfers between devices  97.9 us (31%)
  blocking collectives  69.7 us (22%)
  other arithmetic  68.5 us (22%)
  local copies, waits for them, and re-layouts  44.3 us (14%)
  between operations  15 us (5%)
  matrix products  14 us (5%)
    all_gather x1, waiting for transfers between devices, per_device(): lax.all_gather(front_blocks, 'dom', axis=0, tiled=True)  56.3 us
    all_gather x1, waiting for transfers between devices, per_device(): lax.all_gather(node_blocks, 'dom', axis=0, tiled=True)  41.6 us
    reduce_sum x8, other arithmetic, one_block(): degree = jnp.sum(dense_rows, axis=1).astype(jnp.float32)  28.7 us
    gather x4, local copies, waits for them, and re-layouts, pick_blocks(): jnp.take(arriving, jnp.clip(wanted, 0, arriving.shape[0] - 1), axis=0)  25.7 us
    all_to_all x1, blocking collectives, from_everyone(): return lax.all_to_all(copies, axis, split_axis=0, concat_axis=0, tiled=True)  23.8 us
    convert_element_type x8, other arithmetic, one_block(): dense_rows.astype(jnp.bfloat16)  22.2 us
    all_to_all x1, blocking collectives, sent_and_summed(): lax.all_to_all(in_blocks(shard, dim, devices), axis, 0, 0, tiled=True)  19.6 us
    select_n x2, other arithmetic, pick_blocks(): return jnp.where(inside[:, None], taken_rows, holding)  13.7 us
  transfers between devices with their start and end apart: 2, of which 2 were waited for; matrix products, arithmetic and copies ran while one was open for 3% of the time, Pallas kernels for 0%

commit v1 on v0

v1 whole, which is shorter than its diff:
```python
import jax
import jax.numpy as jnp
from jax import lax
from jax.experimental import pallas as pl
from jax.experimental.pallas import tpu as pltpu
from jax.sharding import PartitionSpec as P

MESH = pl.DeviceIdType.MESH
BF = jnp.bfloat16
F32 = jnp.float32
I32 = jnp.int32
ROWS = 1024
RB = 256
WORDS = 512
CQ = 43


def lane_groups(count, width, lanes):
    lane = lax.broadcasted_iota(I32, (1, lanes), 1)
    return [
        jnp.where((lane >= j * width) & (lane < (j + 1) * width), 1.0, 0.0).astype(BF)
        for j in range(count)
    ]


def quarter_of(index):
    return sum((index >= CQ * m).astype(I32) for m in range(1, 5))


def ones_at(hit):
    return jnp.where(hit, 1.0, 0.0).astype(BF)


def dot(a, b):
    return jnp.dot(a, b, preferred_element_type=F32)


def kernel(
    need_s, need_v, xs, a1, a2, aq, w, out,
    gx0, gx1, gx2, gx3, gp0, gp1, gp2, a1o, a2o, aqo, wg, need_r, need_o, sx, npk, ng, acc1, nr, acc2, accq,
    lhs, rhs1, rhs2, rhsq, sel1, sel2, wr, hid, pm, rg, lm, lgot,
    rx, ssx, sib1, rp, ssp, sib2, mr, ms, lsem,
):
    gx, gp = (gx0, gx1, gx2, gx3), (gp0, gp1, gp2)
    dom = lax.axis_index("dom")
    b = lax.axis_index("batch")
    c = lax.axis_index("col")
    core = dom % 2
    s1, s2 = 2 + 6 * core, 8 - 6 * core
    p1, p2 = (dom // s1) % 4, (dom // s2) % 4

    def at(d1, d2):
        return dom + s1 * ((p1 + d1) % 4 - p1) + s2 * ((p2 + d2) % 4 - p2)

    sib = dom + 1 - 2 * core
    rel = [
        (1 - b, c, {"col": c, "batch": 1 - b}),
        (b, 1 - c, {"col": 1 - c, "batch": b}),
        (1 - b, 1 - c, {"col": 1 - c, "batch": 1 - b}),
    ]
    q = 2 * c + b
    ts = 2 * b + c

    barrier = pltpu.get_barrier_semaphore()
    for n in (at(1, 0), at(3, 0), at(0, 1), at(0, 3), sib):
        pl.semaphore_signal(barrier, inc=1, device_id={"dom": n}, device_id_type=MESH)
    for _, _, dev in rel:
        pl.semaphore_signal(barrier, inc=1, device_id=dev, device_id_type=MESH)
    pl.semaphore_wait(barrier, 8)

    started = []

    def xchg(k, e, src, dst):
        cp = pltpu.make_async_remote_copy(
            src_ref=src, dst_ref=dst, send_sem=ms.at[k], recv_sem=mr.at[k],
            device_id=rel[e][2], device_id_type=MESH,
        )
        cp.start()
        started.append(cp)
        return cp

    def gather_over_dom(g, chunks, rsem, ssem, bsem, own):
        def copy(t, src, target, rs, first=False):
            pltpu.make_async_remote_copy(
                src_ref=own(t) if first else part(t, src), dst_ref=part(t, src),
                send_sem=ssem.at[t], recv_sem=rs, device_id={"dom": target}, device_id_type=MESH,
            ).start()

        def part(t, src, count=1):
            return g[t].at[pl.ds(pl.multiple_of(8 * src, 8), 8 * count)]

        def slot(t, d1, d2):
            return rsem.at[t, 4 * d1 + d2]

        def arrived(t, d1, d2):
            pltpu.make_async_copy(part(t, 0), part(t, 0), slot(t, d1, d2)).wait()

        def to_sib(t, d1, d2):
            copy(t, at(d1, d2), sib, bsem.at[t])

        def spread(t, d1):
            copy(t, at(d1, 0), at(0, 1), slot(t, d1, 3))
            copy(t, at(d1, 0), at(0, 3), slot(t, d1, 1))

        def pass_on(t, d1):
            f = 3 - 2 * ((t + d1) % 2)
            copy(t, at(d1, f), at(0, 4 - f), slot(t, d1, 2))

        def stage_a(t):
            copy(t, dom, at(1, 0), slot(t, 3, 0), True)
            copy(t, dom, at(3, 0), slot(t, 1, 0), True)
            copy(t, dom, at(0, 1), slot(t, 0, 3), True)
            copy(t, dom, at(0, 3), slot(t, 0, 1), True)
            copy(t, dom, sib, bsem.at[t], True)

        def stage_b(t):
            for d1 in (1, 3):
                arrived(t, d1, 0)
                spread(t, d1)
            f = 3 - 2 * (t % 2)
            copy(t, at(f, 0), at(4 - f, 0), slot(t, 2, 0))
            for d2 in (1, 3):
                arrived(t, 0, d2)
            pass_on(t, 0)
            for d in (1, 3):
                to_sib(t, d, 0)
                to_sib(t, 0, d)

        def stage_c(t):
            arrived(t, 2, 0)
            spread(t, 2)
            for d1 in (1, 3):
                arrived(t, d1, 1)
                arrived(t, d1, 3)
                pass_on(t, d1)
            arrived(t, 0, 2)
            to_sib(t, 2, 0)
            to_sib(t, 0, 2)
            for d1 in (1, 3):
                to_sib(t, d1, 1)
                to_sib(t, d1, 3)

        def stage_d(t):
            arrived(t, 2, 1)
            arrived(t, 2, 3)
            pass_on(t, 2)
            for d in (1, 3):
                arrived(t, d, 2)
                to_sib(t, d, 2)
                to_sib(t, 2, d)

        def stage_e(t):
            arrived(t, 2, 2)
            to_sib(t, 2, 2)

        def done(t):
            half = part(t, 0, 16)
            pltpu.make_async_copy(half, half, bsem.at[t]).wait()

        def drain(t):
            most = part(t, 0, 31)
            pltpu.make_async_copy(most, most, ssem.at[t]).wait()

        def run(stage):
            for t in range(chunks):
                stage(t)

        return run, (stage_a, stage_b, stage_c, stage_d, stage_e), done, drain

    mine = pl.ds(pl.multiple_of(8 * dom, 8), 8)
    run1, st1, done1, drain1 = gather_over_dom(gx, 4, rx, ssx, sib1, lambda t: xs.at[t, b])
    run2, st2, done2, drain2 = gather_over_dom(gp, 3, rp, ssp, sib2, lambda t: gp[t].at[mine])

    c_need = xchg(3, 0, need_v, need_r)
    run1(st1[0])
    h = pl.ds(0, 512), pl.ds(512, 512)
    c_a1 = [xchg(4, 0, a1.at[h[0]], a1o.at[h[0]]), xchg(5, 2, a1.at[h[1]], a1o.at[h[1]])]
    c_self = xchg(10, 1, xs.at[2 * b + 1 - c], sx.at[pl.ds(2 * c, 2)])
    c_w = [xchg(k, k, w, wg.at[q]) for k in range(3)]
    c_a2 = [
        xchg(6, 0, a2.at[h[0]], a2o.at[h[0]]), xchg(7, 2, a2.at[h[1]], a2o.at[h[1]]),
        xchg(8, 0, aq.at[h[0]], aqo.at[h[0]]), xchg(9, 2, aq.at[h[1]], aqo.at[h[1]]),
    ]
    for t in range(4):
        gx[t][mine] = xs[t, b]
    wg[q] = w[...]
    sx[pl.ds(2 * c, 2)] = xs[ts]

    c_need.wait_recv()
    to_smem = pltpu.make_async_copy(need_r, need_o, lsem)
    to_smem.start()
    to_smem.wait()

    for stage in st1[1:]:
        run1(stage)

    lists = (need_s, need_o)

    def pick(load, listed, row, dst):
        def body(p, _):
            halves = []
            for e in range(2):
                g = listed[row, 2 * p + e]
                v = load(lax.shift_right_logical(g, 1)).astype(F32)
                odd = (g & 1).astype(F32)
                halves.append(v[0:8] * (1.0 - odd) + v[8:16] * odd)
            dst[pl.ds(pl.multiple_of(p * 16, 16), 16), :] = jnp.concatenate(halves, 0).astype(BF)
            return 0

        lax.fori_loop(0, 32, body, 0)

    m32 = lane_groups(4, 32, 128)
    bases = (b * ROWS, (1 - b) * ROWS)
    ones = jnp.ones((WORDS, 128), BF)
    zero_bf, one_bf = jnp.zeros((), BF), jnp.ones((), BF)

    def hot(a, bit):
        return jnp.where(a == jnp.asarray(2.0 ** bit, BF), one_bf, zero_bf)

    for t in range(4):
        done1(t)
        for s in range(2):
            if t == 0 and s == 1:
                for cp in c_a1:
                    cp.wait_recv()
            adj = (a1, a1o)[s]
            pick(lambda i, t=t: gx[t][i], lists[s], 0, sel1)
            picked = sel1[...]
            for j in range(4):
                rhs1[j * WORDS : (j + 1) * WORDS, :] = picked * m32[j]

            def rows(i, _, t=t, s=s, adj=adj):
                a = adj[pl.ds(pl.multiple_of(i * RB, RB), RB), :]
                for j in range(4):
                    lhs[:, j * WORDS : (j + 1) * WORDS] = hot(a, 4 * t + j)
                part = dot(lhs[:, : 4 * WORDS], rhs1[...])
                at_rows = pl.ds(pl.multiple_of(bases[s] + i * RB, RB), RB)
                if t == 0:
                    acc1[at_rows, :] = part
                else:
                    acc1[at_rows, :] += part
                return 0

            lax.fori_loop(0, ROWS // RB, rows, 0)

    for s in range(2):
        adj = (a1, a1o)[s]

        def mean(i, _, s=s, adj=adj):
            a = adj[pl.ds(pl.multiple_of(i * RB, RB), RB), :]
            deg = dot(jnp.where(a != zero_bf, one_bf, zero_bf), ones)
            at_rows = pl.ds(pl.multiple_of(bases[s] + i * RB, RB), RB)
            x = acc1[at_rows, :]
            x = x + pltpu.roll(x, 32, 1)
            x = x + pltpu.roll(x, 64, 1)
            nr[at_rows, :] = x / jnp.maximum(deg, 1.0)
            return 0

        lax.fori_loop(0, ROWS // RB, mean, 0)

    lane = lax.broadcasted_iota(I32, (128, 128), 1)
    for t in range(4):
        x = nr[pl.ds(4 * t, 128, stride=16), :]
        for j in range(1, 4):
            x = jnp.where(lane >= 32 * j, nr[pl.ds(4 * t + j, 128, stride=16), :], x)
        npk[t] = x.astype(BF)
    c_near = [
        xchg(11 + e, e, npk.at[2 * rel[e][0] + rel[e][1]], ng.at[q]) for e in range(3)
    ]
    ng[q] = npk[ts]

    for cp in c_w:
        cp.wait_recv()
    for k in range(2):
        for cc in range(2):
            for bb in range(2):
                for qb in range(2):
                    piece = wg[2 * cc + bb, 64 * k + 32 * qb : 64 * k + 32 * qb + 32, :]
                    for j in range(4):
                        r0 = (2 * cc + qb) * 128 + j * 32
                        wr[k, r0 : r0 + 32, 128 * bb : 128 * bb + 128] = piece
    c_self.wait_recv()
    for cp in c_near:
        cp.wait_recv()
    for j in range(4):
        ls = jnp.concatenate([sx[i].reshape(128, 128) * m32[j] for i in range(4)], 1)
        ln = jnp.concatenate([ng[i] * m32[j] for i in range(4)], 1)
        hid[j] = jnp.maximum(dot(ls, wr[0]) + dot(ln, wr[1]), 0.0).astype(BF)

    low = lax.broadcasted_iota(I32, (256, 128), 1) < 64
    for k in range(2):
        for bb in range(2):
            r0 = 256 - 128 * k
            v = jnp.concatenate([wg[bb, r0 : r0 + 128, :], wg[2 + bb, r0 : r0 + 128, :]], 0)
            v = v.astype(F32)
            turned = pltpu.roll(v, 64, 1)
            for hh in range(2):
                fit, swap = (v, turned) if hh == 0 else (turned, v)
                wa = jnp.where(low, fit, 0.0).astype(BF)
                wb = jnp.where(low, 0.0, swap).astype(BF)
                for jj in range(2):
                    x = dot(hid[2 * jj], wa) + dot(hid[2 * jj + 1], wb)
                    pm[2 * bb + hh, 2 * k + jj] = x.astype(BF)
    c_p = [
        xchg(14 + e, e, pm.at[2 * rel[e][0] + rel[e][1], pl.ds(0, 2)], rg.at[ts, pl.ds(0, 2)])
        for e in range(3)
    ]
    c_q = [
        xchg(17 + e, e, pm.at[2 * rel[e][0] + rel[e][1], pl.ds(2, 2)], rg.at[ts, pl.ds(2, 2)])
        for e in range(3)
    ]
    rg[ts] = pm[ts]
    for cp in c_p:
        cp.wait_recv()
    for u in range(3):
        t0 = (0, 2, 5)[u]
        tiles = jnp.concatenate([rg[i // 2, i % 2] for i in range(t0, t0 + 3)], 1)
        l = lax.broadcasted_iota(I32, (384, 256), 1)
        r = lax.broadcasted_iota(I32, (384, 256), 0)
        j = quarter_of(l)
        goal = (5 * u + j) * 64 + l - CQ * j - 128 * t0
        x = dot(tiles, ones_at((r == goal) & (l < 5 * CQ))).astype(BF)
        for tile in range(2):
            gp[u][mine, tile] = x[:, 128 * tile : 128 * tile + 128].reshape(8, 16, 128)

    for stage in st2:
        run2(stage)

    for cp in c_q:
        cp.wait_recv()
    m64 = lane_groups(2, 64, 128)
    for i in range(16):
        rhsq[i * 128 : (i + 1) * 128, :] = rg[i // 4, 2 + (i % 4) // 2] * m64[i % 2]
    for cp in c_a2:
        cp.wait_recv()
    for s in range(2):
        own = (aq, aqo)[s]

        def own_rows(i, _, s=s, own=own):
            a = own[pl.ds(pl.multiple_of(i * RB, RB), RB), :]
            for j in range(16):
                lhs[:, j * 128 : (j + 1) * 128] = hot(a, j)
            accq[pl.ds(pl.multiple_of(s * ROWS + i * RB, RB), RB), :] = dot(lhs[:, :2048], rhsq[...])
            return 0

        lax.fori_loop(0, ROWS // RB, own_rows, 0)

    m43 = lane_groups(5, CQ, 256)
    for u in range(3):
        done2(u)
        for s in range(2):
            adj = (a2, a2o)[s]
            for tile in range(2):
                pick(lambda i, u=u, tile=tile: gp[u][i, tile], lists[s], 1, sel2.at[tile])
            picked = jnp.concatenate([sel2[0], sel2[1]], 1)
            for j in range(5):
                rhs2[j * WORDS : (j + 1) * WORDS, :] = picked * m43[j]

            def rows2(i, _, u=u, s=s, adj=adj):
                a = adj[pl.ds(pl.multiple_of(i * RB, RB), RB), :]
                for j in range(5):
                    lhs[:, j * WORDS : (j + 1) * WORDS] = hot(a, 5 * u + j)
                part = dot(lhs[...], rhs2[...])
                at_rows = pl.ds(pl.multiple_of(s * ROWS + i * RB, RB), RB)
                if u == 0:
                    acc2[at_rows, :] = part
                else:
                    acc2[at_rows, :] += part
                return 0

            lax.fori_loop(0, ROWS // RB, rows2, 0)

    l = lax.broadcasted_iota(I32, (256, 128), 0)
    m = lax.broadcasted_iota(I32, (256, 128), 1)
    cls = l - CQ * quarter_of(l)
    fold = [ones_at((m == cls + 64 * hh) & (l < 5 * CQ)) for hh in range(2)]
    fold = [jnp.concatenate([f, f], 0) for f in fold]
    low = lax.broadcasted_iota(I32, (RB, 128), 1) < 64
    for s in (1, 0):
        adj = (a2, a2o)[s]

        def close(i, _, s=s, adj=adj):
            res, own = [], []
            for hh in range(2):
                r0 = pl.multiple_of(512 * hh + i * RB, RB)
                a = adj[pl.ds(r0, RB), :]
                deg = dot(jnp.where(a != zero_bf, one_bf, zero_bf), ones)
                deg = jnp.maximum(deg, 1.0)
                at_rows = pl.ds(pl.multiple_of(s * ROWS + r0, RB), RB)
                x = acc2[at_rows, :] / jnp.concatenate([deg, deg], 1)
                top = x.astype(BF)
                rest = (x - top.astype(F32)).astype(BF)
                res.append(dot(jnp.concatenate([top, rest], 1), fold[hh]))
                y = accq[at_rows, :]
                own.append(y + pltpu.roll(y, 64, 1))
            total = res[0] + res[1] + jnp.where(low, own[0], own[1])
            lm[s, pl.ds(pl.multiple_of(i * RB, RB), RB), :] = total.astype(BF)
            return 0

        lax.fori_loop(0, 2, close, 0)
        if s == 1:
            c_l = [xchg(20, 0, lm.at[1], lgot.at[ts]), xchg(22, 2, lm.at[1], lgot.at[ts])]
    c_l.append(xchg(21, 1, lm.at[0], lgot.at[ts]))
    lgot[ts] = lm[0]
    for cp in c_l:
        cp.wait_recv()
    n = lax.broadcasted_iota(I32, (512, 256), 1)
    r = lax.broadcasted_iota(I32, (512, 256), 0)
    k = quarter_of(n)
    goal = 128 * k + n - CQ * k
    got = jnp.concatenate([lgot[i] for i in range(4)], 1)
    for hh in range(2):
        out[512 * hh : 512 * hh + 512, :] = dot(got, ones_at(r == goal + 64 * hh))[:, :172]

    for t in range(4):
        drain1(t)
    for t in range(3):
        drain2(t)
    for cp in started:
        cp.wait_send()


def per_device(
    features, self_weight1, neigh_weight1, need_first, count_first, adjacency_first,
    self_weight2, neigh_weight2, need_second, count_second, adjacency_second, seed_rows,
):
    xs = features.reshape(128, 4, 4, 2, 32).transpose(1, 3, 0, 2, 4).reshape(4, 2, 8, 16, 128)
    word = lax.broadcasted_iota(I32, (ROWS, WORDS), 1)
    a1 = jnp.where(word < 8 * count_first[0], adjacency_first, 0).astype(BF)
    a2 = jnp.where(word < 8 * count_second[0], adjacency_second, 0).astype(BF)
    own_word = lax.broadcasted_iota(I32, (ROWS, 128), 1)
    bit = jnp.left_shift(1, seed_rows % 16)
    aq = jnp.where(own_word == (seed_rows // 16)[:, None], bit[:, None], 0).astype(BF)
    needs = jnp.zeros((8, 128), I32).at[0, :64].set(need_first[0]).at[1, :64].set(need_second[0])

    def classes(x):
        return jnp.pad(x.reshape(128, 2, CQ), ((0, 0), (0, 0), (0, 64 - CQ))).reshape(128, 128)

    w = jnp.concatenate(
        [self_weight1, neigh_weight1, classes(self_weight2), classes(neigh_weight2)], 0
    )
    vm = pl.BlockSpec(memory_space=pltpu.VMEM)
    sm = pl.BlockSpec(memory_space=pltpu.SMEM)
    dma = pltpu.SemaphoreType.DMA
    return pl.pallas_call(
        kernel,
        out_shape=jax.ShapeDtypeStruct((ROWS, 172), F32),
        in_specs=[sm] + [vm] * 6,
        out_specs=vm,
        scratch_shapes=[
            *[pltpu.VMEM((256, 16, 128), BF)] * 4,
            *[pltpu.VMEM((256, 2, 16, 128), BF)] * 3,
            pltpu.VMEM((ROWS, WORDS), BF),
            pltpu.VMEM((ROWS, WORDS), BF),
            pltpu.VMEM((ROWS, 128), BF),
            pltpu.VMEM((4, 384, 128), BF),
            pltpu.VMEM((8, 128), I32),
            pltpu.SMEM((8, 128), I32),
            pltpu.VMEM((4, 8, 16, 128), BF),
            pltpu.VMEM((4, 128, 128), BF),
            pltpu.VMEM((4, 128, 128), BF),
            pltpu.VMEM((2 * ROWS, 128), F32),
            pltpu.VMEM((2 * ROWS, 128), F32),
            pltpu.VMEM((2 * ROWS, 256), F32),
            pltpu.VMEM((2 * ROWS, 128), F32),
            pltpu.VMEM((RB, 5 * WORDS), BF),
            pltpu.VMEM((4 * WORDS, 128), BF),
            pltpu.VMEM((5 * WORDS, 256), BF),
            pltpu.VMEM((2048, 128), BF),
            pltpu.VMEM((WORDS, 128), BF),
            pltpu.VMEM((2, WORDS, 128), BF),
            pltpu.VMEM((2, 512, 256), BF),
            pltpu.VMEM((4, 128, 256), BF),
            pltpu.VMEM((4, 4, 128, 128), BF),
            pltpu.VMEM((4, 4, 128, 128), BF),
            pltpu.VMEM((2, 512, 128), BF),
            pltpu.VMEM((4, 512, 128), BF),
            dma((4, 16)), dma((4,)), dma((4,)),
            dma((3, 16)), dma((3,)), dma((3,)),
            dma((23,)), dma((23,)), dma(()),
        ],
        compiler_params=pltpu.CompilerParams(
            collective_id=0, has_side_effects=True, vmem_limit_bytes=60 * 2**20
        ),
    )(needs, needs, xs, a1, a2, aq, w)


def solution(mesh):
    both = P(("dom", "batch"))
    rows = P(("dom", "batch"), None)
    wide = P("col", "batch")
    placed = (
        P("dom", "col"), wide, wide, rows, both, rows, wide, wide, rows, both, rows, both,
    )
    return jax.shard_map(
        per_device, mesh=mesh, in_specs=placed, out_specs=rows, check_vma=False
    )
```

time: 311 us -> 126 us (0.41)
  Pallas kernels: 0 us -> 109 us
  waiting for transfers between devices: 97.9 us -> 0 us
  blocking collectives: 69.7 us -> 0 us
  other arithmetic: 68.5 us -> 7.31 us
  local copies, waits for them, and re-layouts: 44.3 us -> 8.66 us
  matrix products: 14 us -> 0 us
  between operations: 15 us -> 1.38 us
    pallas_call x0 -> x1, Pallas kernels: none -> 109 us  [per_device(): pl.pallas_call(kernel, out_shape=jax.ShapeDtypeStruct((ROWS, 172), F32),...]
    all_gather x2 -> x0, waiting for transfers between devices: 97.9 us -> none  [the longest x1 56.3 us: per_device(): lax.all_gather(front_blocks, 'dom', axis=0, tiled=True)]
    all_to_all x2 -> x0, blocking collectives: 43.3 us -> none  [the longest x1 23.8 us: from_everyone(): return lax.all_to_all(copies, axis, split_axis=0, concat_axis=0, tiled=True)]
    reduce_sum x10 -> x0, other arithmetic: 29.8 us -> none  [the longest x8 28.7 us: one_block(): degree = jnp.sum(dense_rows, axis=1).astype(jnp.float32)]
    gather x5 -> x0, local copies, waits for them, and re-layouts: 28.9 us -> none  [the longest x4 25.7 us: pick_blocks(): jnp.take(arriving, jnp.clip(wanted, 0, arriving.shape[0] - 1), axis=0)]
    all_gather x5 -> x0, blocking collectives: 26.4 us -> none  [the longest x1 7.99 us: per_device(): frontier = lax.all_gather(hidden_first, 'batch', axis=0, tiled=True)]
    convert_element_type x9 -> x2, other arithmetic: 22.3 us -> 5.18 us  [the longest x1 4.14 us: per_device(): a2 = jnp.where(word < 8 * count_second[0], adjacency_second, 0).astype(BF)]
    dot_general x12 -> x0, matrix products: 14 us -> none  [the longest x8 9.44 us: one_block(): jnp.dot(dense_rows.astype(jnp.bfloat16), needed, preferred_element_type=j...]
  transfers between devices with their start and end apart: 2 -> 0, of which waited for: 2 -> 0; matrix products, arithmetic and copies ran while one was open for 3% -> 0% of each run, Pallas kernels for 0% -> 0%
where the time goes in v1:
time: 126 us
  Pallas kernels  109 us (87%)
  local copies, waits for them, and re-layouts  8.66 us (7%)
  other arithmetic  7.31 us (6%)
  between operations  1.38 us (1%)
    pallas_call x1, Pallas kernels, per_device(): pl.pallas_call(kernel, out_shape=jax.ShapeDtypeStruct((ROWS, 172), F32),...  109 us
    convert_element_type x1, other arithmetic, per_device(): a2 = jnp.where(word < 8 * count_second[0], adjacency_second, 0).astype(BF)  4.14 us

profile of v1, /device:TPU:0, one launch (start us, length us, event | category | flops | bytes accessed | tf_op | source)
XLA Modules:
  0.0 126.0 jit_solution(12731732760001417265)
XLA Ops:
  1.3 0.7 scatter.6
  2.0 0.7 scatter.9.need_s.need_v
  2.7 0.0 copy-start
  2.7 0.7 add_select_fusion.1
  3.4 0.7 reshape.82
  4.2 0.1 copy.19
  4.3 0.8 reshape.84
  5.1 0.1 copy.20
  5.2 1.4 %pad_maximum_fusion.w = bf16[384,128]{1,0:T(8,128)(2,1)} fusion(bf16[128,128]{1,0:T(8,128)(2,1)S(1)} %copy.20, bf16[128,128]{1,0:T(8,128)(2,1)S(1)} %copy.19, bf16[64,128]{1,0:T(8,128)(2,1)} %param.18, bf16[64,128]{1,0:T(8,128)(2,1)} %param.17), kind=kLoop, calls=%fused_computation.4 | loop fusion | flops 393216 | bytes 196608 | tf_op jit(solution)/shard_map/concatenate | solution.py:439
  6.6 1.0 select_convert_fusion.2.aq
  7.6 1.2 copy.17
  8.9 0.4 reshape.80
  9.3 0.3 copy.18
  9.6 0.0 copy-done
  9.6 1.2 reshape.81.xs
  10.8 4.1 %select_convert_fusion = (bf16[1024,512]{1,0:T(8,128)(2,1)}, bf16[1024,512]{1,0:T(8,128)(2,1)}) fusion(s32[1024,512]{1,0:T(8,128)} %param.26, pred[512]{0:T(512)(128)(4,1)S(1)} %iota_compare_fusion.1, s32[1024,512]{1,0:T(8,128)} %param.21, pred[512]{0:T(512)(128)(4,1)S(1)} %iota_compare_fusion.2), kind=kLoop, calls=%fused_computation | loop fusion | flops 2097152 | bytes 6292480 | tf_op jit(solution)/shard_map/convert_element_type | solution.py:430
  14.9 108.7 %shard_map.118 = f32[1024,172]{1,0:T(8,128)} custom-call(s32[8,128]{1,0:T(8,128)} %copy-done, s32[8,128]{1,0:T(8,128)} %copy-done, bf16[4,2,8,16,128]{4,3,2,1,0:T(8,128)(2,1)} %reshape.81.xs, bf16[1024,512]{1,0:T(8,128)(2,1)} %get-tuple-element.32.a1, bf16[1024,512]{1,0:T(8,128)(2,1)} %get-tuple-element.31.a2, bf16[1024,128]{1,0:T(8,128)(2,1)} %select_convert_fusion.2.aq, ...), custom_call_target="tpu_custom_call" | custom-call | tf_op jit(solution)/shard_map/pallas_call | solution.py:445
  123.6 2.4 %copy.21 = f32[1024,172]{0,1:T(8,128)} copy(f32[1024,172]{1,0:T(8,128)} %shard_map.118) | data formatting | bytes 1409024 | tf_op jit(solution)/shard_map/pallas_call | solution.py:445
  (4 shorter events, 0.0 us)
Async XLA Ops:
  2.7 6.8 %copy-start = (s32[8,128]{1,0:T(8,128)}, s32[8,128]{1,0:T(8,128)S(1)}, u32[]{:S(2)}) copy-start(s32[8,128]{1,0:T(8,128)S(1)} %scatter.9.need_s.need_v) | copy-start | bytes 12292

commit v2 on v1

--- a/solution.py
+++ b/solution.py
@@ -10,7 +10,8 @@
 F32 = jnp.float32
 I32 = jnp.int32
 ROWS = 1024
-RB = 256
+RB = 512
+HB = 256
 WORDS = 512
 CQ = 43
 
@@ -36,9 +37,10 @@
 
 
 def kernel(
-    need_s, need_v, xs, a1, a2, aq, w, out,
-    gx0, gx1, gx2, gx3, gp0, gp1, gp2, a1o, a2o, aqo, wg, need_r, need_o, sx, npk, ng, acc1, nr, acc2, accq,
-    lhs, rhs1, rhs2, rhsq, sel1, sel2, wr, hid, pm, rg, lm, lgot,
+    need1_s, need2_s, count1, count2, need1_v, need2_v, feats, w1s, w1n, w2s, w2n, seeds,
+    adj1, adj2, out, xs, a1, a2, aq, w, raw1, raw2, fx, wt,
+    gx0, gx1, gx2, gx3, gp0, gp1, gp2, a1o, a2o, aqo, wg, need1_r, need2_r, need1_o, need2_o, sx, npk, ng, acc1, nr, acc2, accq,
+    lhs, rhs1, rhs2, rhsq, wr, hid, pm, rg, lm, lgot,
     rx, ssx, sib1, rp, ssp, sib2, mr, ms, lsem,
 ):
     gx, gp = (gx0, gx1, gx2, gx3), (gp0, gp1, gp2)
@@ -61,11 +63,28 @@
     q = 2 * c + b
     ts = 2 * b + c
 
+    load1 = pltpu.make_async_copy(adj1, raw1, lsem.at[0])
+    load2 = pltpu.make_async_copy(adj2, raw2, lsem.at[1])
+    load1.start()
+    load2.start()
     barrier = pltpu.get_barrier_semaphore()
     for n in (at(1, 0), at(3, 0), at(0, 1), at(0, 3), sib):
         pl.semaphore_signal(barrier, inc=1, device_id={"dom": n}, device_id_type=MESH)
     for _, _, dev in rel:
         pl.semaphore_signal(barrier, inc=1, device_id=dev, device_id_type=MESH)
+    for i in range(16):
+        cut = slice(128 * i, 128 * i + 128)
+        fx[cut, :64] = feats[:, cut].astype(F32).T
+    lane = lax.broadcasted_iota(I32, (128, 128), 1)
+    for t in range(4):
+        parts = [fx[pl.ds(4 * t + j, 128, stride=16), :] for j in range(4)]
+        for qb in range(2):
+            x = parts[0] if qb == 0 else pltpu.roll(parts[0], 96, 1)
+            for j in range(1, 4):
+                turn = (32 * j - 32 * qb) % 128
+                moved = pltpu.roll(parts[j], turn, 1) if turn else parts[j]
+                x = jnp.where(lane >= 32 * j, moved, x)
+            xs[t, qb] = x.astype(BF).reshape(8, 16, 128)
     pl.semaphore_wait(barrier, 8)
 
     started = []
@@ -161,21 +180,47 @@
             most = part(t, 0, 31)
             pltpu.make_async_copy(most, most, ssem.at[t]).wait()
 
-        def run(stage):
-            for t in range(chunks):
-                stage(t)
-
-        return run, (stage_a, stage_b, stage_c, stage_d, stage_e), done, drain
+        stages = dict(a=stage_a, b=stage_b, c=stage_c, d=stage_d, e=stage_e, f=done)
+
+        def run(order):
+            for kind, t in zip(order[::2], order[1::2]):
+                stages[kind](int(t))
+
+        return run, drain
 
     mine = pl.ds(pl.multiple_of(8 * dom, 8), 8)
-    run1, st1, done1, drain1 = gather_over_dom(gx, 4, rx, ssx, sib1, lambda t: xs.at[t, b])
-    run2, st2, done2, drain2 = gather_over_dom(gp, 3, rp, ssp, sib2, lambda t: gp[t].at[mine])
-
-    c_need = xchg(3, 0, need_v, need_r)
-    run1(st1[0])
+    run1, drain1 = gather_over_dom(gx, 4, rx, ssx, sib1, lambda t: xs.at[t, b])
+    run2, drain2 = gather_over_dom(gp, 3, rp, ssp, sib2, lambda t: gp[t].at[mine])
+
+    c_need = [xchg(3, 0, need1_v, need1_r), xchg(21, 0, need2_v, need2_r)]
+    run1("a0a1a2a3")
     h = pl.ds(0, 512), pl.ds(512, 512)
+    c_self = xchg(10, 1, xs.at[2 * b + 1 - c], sx.at[pl.ds(2 * c, 2)])
+
+    def words(load, raw, count, dst):
+        load.wait()
+        word = lax.broadcasted_iota(I32, (128, WORDS), 1)
+        limit = 8 * count[0]
+        for i in range(8):
+            cut = slice(128 * i, 128 * i + 128)
+            dst[cut, :] = jnp.where(word < limit, raw[cut, :], 0).astype(F32).astype(BF)
+
+    words(load1, raw1, count1, a1)
     c_a1 = [xchg(4, 0, a1.at[h[0]], a1o.at[h[0]]), xchg(5, 2, a1.at[h[1]], a1o.at[h[1]])]
-    c_self = xchg(10, 1, xs.at[2 * b + 1 - c], sx.at[pl.ds(2 * c, 2)])
+    w[0:64] = w1s[...]
+    w[64:128] = w1n[...]
+    for k, x in enumerate((w2s, w2n)):
+        wt[...] = jnp.zeros_like(wt)
+        wt[0:CQ, :] = x[0:CQ, :].astype(F32)
+        wt[64 : 64 + CQ, :] = x[CQ : 2 * CQ, :].astype(F32)
+        w[128 + 128 * k : 256 + 128 * k] = wt[...].T.astype(BF)
+    words(load2, raw2, count2, a2)
+    row = lax.broadcasted_iota(I32, (128, 128), 0)
+    for i in range(8):
+        seed = seeds[i : i + 1, :]
+        bit = jnp.left_shift(jnp.ones_like(seed), seed & 15)
+        own = jnp.where(row == lax.shift_right_logical(seed, 4), bit, 0)
+        aq[128 * i : 128 * i + 128, :] = own.astype(F32).T.astype(BF)
     c_w = [xchg(k, k, w, wg.at[q]) for k in range(3)]
     c_a2 = [
         xchg(6, 0, a2.at[h[0]], a2o.at[h[0]]), xchg(7, 2, a2.at[h[1]], a2o.at[h[1]]),
@@ -186,28 +231,32 @@
     wg[q] = w[...]
     sx[pl.ds(2 * c, 2)] = xs[ts]
 
-    c_need.wait_recv()
-    to_smem = pltpu.make_async_copy(need_r, need_o, lsem)
-    to_smem.start()
-    to_smem.wait()
-
-    for stage in st1[1:]:
-        run1(stage)
-
-    lists = (need_s, need_o)
-
-    def pick(load, listed, row, dst):
-        def body(p, _):
-            halves = []
-            for e in range(2):
-                g = listed[row, 2 * p + e]
-                v = load(lax.shift_right_logical(g, 1)).astype(F32)
-                odd = (g & 1).astype(F32)
-                halves.append(v[0:8] * (1.0 - odd) + v[8:16] * odd)
-            dst[pl.ds(pl.multiple_of(p * 16, 16), 16), :] = jnp.concatenate(halves, 0).astype(BF)
-            return 0
-
-        lax.fori_loop(0, 32, body, 0)
+    rhs2[...] = jnp.zeros_like(rhs2)
+    run1("b0b1b2b3c0c1c2c3d0d1e0f0")
+    for cp in c_need:
+        cp.wait_recv()
+    to_smem = [
+        pltpu.make_async_copy(need1_r, need1_o, lsem.at[2]),
+        pltpu.make_async_copy(need2_r, need2_o, lsem.at[3]),
+    ]
+    for cp in to_smem:
+        cp.start()
+    for cp in to_smem:
+        cp.wait()
+
+    lists1, lists2 = (need1_s, need1_o), (need2_s, need2_o)
+
+    def picked(load, listed, p):
+        halves = []
+        for e in range(2):
+            g = listed[0, 2 * p + e]
+            v = load(lax.shift_right_logical(g, 1)).astype(F32)
+            odd = (g & 1).astype(F32)
+            halves.append(v[0:8] * (1.0 - odd) + v[8:16] * odd)
+        return jnp.concatenate(halves, 0).astype(BF)
+
+    def word_rows(j, p):
+        return pl.ds(pl.multiple_of(j * WORDS + p * 16, 16), 16)
 
     m32 = lane_groups(4, 32, 128)
     bases = (b * ROWS, (1 - b) * ROWS)
@@ -217,31 +266,46 @@
     def hot(a, bit):
         return jnp.where(a == jnp.asarray(2.0 ** bit, BF), one_bf, zero_bf)
 
-    for t in range(4):
-        done1(t)
-        for s in range(2):
-            if t == 0 and s == 1:
-                for cp in c_a1:
-                    cp.wait_recv()
-            adj = (a1, a1o)[s]
-            pick(lambda i, t=t: gx[t][i], lists[s], 0, sel1)
-            picked = sel1[...]
-            for j in range(4):
-                rhs1[j * WORDS : (j + 1) * WORDS, :] = picked * m32[j]
-
-            def rows(i, _, t=t, s=s, adj=adj):
-                a = adj[pl.ds(pl.multiple_of(i * RB, RB), RB), :]
-                for j in range(4):
-                    lhs[:, j * WORDS : (j + 1) * WORDS] = hot(a, 4 * t + j)
-                part = dot(lhs[:, : 4 * WORDS], rhs1[...])
-                at_rows = pl.ds(pl.multiple_of(bases[s] + i * RB, RB), RB)
-                if t == 0:
-                    acc1[at_rows, :] = part
-                else:
-                    acc1[at_rows, :] += part
-                return 0
-
-            lax.fori_loop(0, ROWS // RB, rows, 0)
+    def pick1(unit, k):
+        t, sl = unit
+        for i in range(8):
+            p = 8 * k + i
+            x = picked(lambda n: gx[t][n], lists1[sl], p)
+            for j in range(4 if t < 3 else 3):
+                rhs1[sl, word_rows(j, p), :] = x * m32[j]
+
+    def loop(n, step):
+        def body(k, _):
+            step(k)
+            return 0
+
+        lax.fori_loop(0, n, body, 0)
+
+    loop(4, lambda k: pick1((0, 0), k))
+    units = [(t, sl) for t in range(4) for sl in range(2)]
+    after = ["d2e1f1", "d3e2f2", "e3f3"] + [""] * 5
+    for n, (t, sl) in enumerate(units):
+        if n == 1:
+            for cp in c_a1:
+                cp.wait_recv()
+
+        def rows(i, n=n, t=t, sl=sl):
+            a = (a1, a1o)[sl][pl.ds(pl.multiple_of(i * RB, RB), RB), :]
+            depth = WORDS * (4 if t < 3 else 3)
+            for j in range(depth // WORDS):
+                lhs[:, j * WORDS : (j + 1) * WORDS] = hot(a, 4 * t + j)
+            if n < 7:
+                for k in range(2):
+                    pick1(units[n + 1], 2 * i + k)
+            part = dot(lhs[:, :depth], rhs1[sl, :depth, :])
+            at_rows = pl.ds(pl.multiple_of(bases[sl] + i * RB, RB), RB)
+            if t == 0:
+                acc1[at_rows, :] = part
+            else:
+                acc1[at_rows, :] += part
+
+        loop(2, rows)
+        run1(after[n])
 
     for s in range(2):
         adj = (a1, a1o)[s]
@@ -323,8 +387,7 @@
         for tile in range(2):
             gp[u][mine, tile] = x[:, 128 * tile : 128 * tile + 128].reshape(8, 16, 128)
 
-    for stage in st2:
-        run2(stage)
+    run2("a0a1a2b0b1b2")
 
     for cp in c_q:
         cp.wait_recv()
@@ -344,73 +407,72 @@
             return 0
 
         lax.fori_loop(0, ROWS // RB, own_rows, 0)
+        run2("c0c1" if s == 0 else "c2d0e0d1f0")
 
     m43 = lane_groups(5, CQ, 256)
-    for u in range(3):
-        done2(u)
-        for s in range(2):
-            adj = (a2, a2o)[s]
+    def pick2(unit, k):
+        u, sl = unit
+        for i in range(8):
+            p = 8 * k + i
             for tile in range(2):
-                pick(lambda i, u=u, tile=tile: gp[u][i, tile], lists[s], 1, sel2.at[tile])
-            picked = jnp.concatenate([sel2[0], sel2[1]], 1)
+                x = picked(lambda n: gp[u][n, tile], lists2[sl], p)
+                cut = slice(128 * tile, 128 * tile + 128)
+                for j in range(2 * tile, 2 * tile + 3):
+                    rhs2[sl, word_rows(j, p), cut] = x * m43[j][:, cut]
+
+    loop(4, lambda k: pick2((0, 0), k))
+    units2 = [(u, sl) for u in range(3) for sl in range(2)]
+    after = ["d2e1f1", "", "e2f2"] + [""] * 3
+    for n, (u, sl) in enumerate(units2):
+
+        def rows2(i, n=n, u=u, sl=sl):
+            a = (a2, a2o)[sl][pl.ds(pl.multiple_of(i * RB, RB), RB), :]
             for j in range(5):
-                rhs2[j * WORDS : (j + 1) * WORDS, :] = picked * m43[j]
-
-            def rows2(i, _, u=u, s=s, adj=adj):
-                a = adj[pl.ds(pl.multiple_of(i * RB, RB), RB), :]
-                for j in range(5):
-                    lhs[:, j * WORDS : (j + 1) * WORDS] = hot(a, 5 * u + j)
-                part = dot(lhs[...], rhs2[...])
-                at_rows = pl.ds(pl.multiple_of(s * ROWS + i * RB, RB), RB)
-                if u == 0:
-                    acc2[at_rows, :] = part
-                else:
-                    acc2[at_rows, :] += part
-                return 0
-
-            lax.fori_loop(0, ROWS // RB, rows2, 0)
-
-    l = lax.broadcasted_iota(I32, (256, 128), 0)
-    m = lax.broadcasted_iota(I32, (256, 128), 1)
-    cls = l - CQ * quarter_of(l)
-    fold = [ones_at((m == cls + 64 * hh) & (l < 5 * CQ)) for hh in range(2)]
-    fold = [jnp.concatenate([f, f], 0) for f in fold]
-    low = lax.broadcasted_iota(I32, (RB, 128), 1) < 64
+                lhs[:, j * WORDS : (j + 1) * WORDS] = hot(a, 5 * u + j)
+            if n < 5:
+                for k in range(2):
+                    pick2(units2[n + 1], 2 * i + k)
+            part = dot(lhs[...], rhs2[sl])
+            at_rows = pl.ds(pl.multiple_of(sl * ROWS + i * RB, RB), RB)
+            if u == 0:
+                acc2[at_rows, :] = part
+            else:
+                acc2[at_rows, :] += part
+
+        loop(2, rows2)
+        run2(after[n])
+
+    l = lax.broadcasted_iota(I32, (48, 256), 1)
+    m = lax.broadcasted_iota(I32, (48, 256), 0)
+    fold = ones_at((m == l - CQ * quarter_of(l)) & (l < 5 * CQ))
+    fold_own = ones_at((m == (l & 63)) & (m < CQ))
+    fold = jnp.concatenate([fold, fold, fold_own], 1)
+    c_l = []
     for s in (1, 0):
         adj = (a2, a2o)[s]
 
-        def close(i, _, s=s, adj=adj):
-            res, own = [], []
-            for hh in range(2):
-                r0 = pl.multiple_of(512 * hh + i * RB, RB)
-                a = adj[pl.ds(r0, RB), :]
-                deg = dot(jnp.where(a != zero_bf, one_bf, zero_bf), ones)
-                deg = jnp.maximum(deg, 1.0)
-                at_rows = pl.ds(pl.multiple_of(s * ROWS + r0, RB), RB)
-                x = acc2[at_rows, :] / jnp.concatenate([deg, deg], 1)
-                top = x.astype(BF)
-                rest = (x - top.astype(F32)).astype(BF)
-                res.append(dot(jnp.concatenate([top, rest], 1), fold[hh]))
-                y = accq[at_rows, :]
-                own.append(y + pltpu.roll(y, 64, 1))
-            total = res[0] + res[1] + jnp.where(low, own[0], own[1])
-            lm[s, pl.ds(pl.multiple_of(i * RB, RB), RB), :] = total.astype(BF)
-            return 0
-
-        lax.fori_loop(0, 2, close, 0)
+        def split(x):
+            top = x.astype(BF)
+            return [top, (x - top.astype(F32)).astype(BF)]
+
+        for i in range(4):
+            a = adj[HB * i : HB * i + HB, :]
+            deg = dot(jnp.where(a != zero_bf, one_bf, zero_bf), ones)
+            deg = jnp.maximum(deg, 1.0)
+            at_rows = slice(s * ROWS + HB * i, s * ROWS + HB * i + HB)
+            x = acc2[at_rows, :] / jnp.concatenate([deg, deg], 1)
+            all_of = jnp.concatenate(split(x) + split(accq[at_rows, :]), 1)
+            lm[s, :, HB * i : HB * i + HB] = lax.dot_general(
+                fold, all_of, (((1,), (1,)), ((), ())), preferred_element_type=F32
+            ).astype(BF)
         if s == 1:
             c_l = [xchg(20, 0, lm.at[1], lgot.at[ts]), xchg(22, 2, lm.at[1], lgot.at[ts])]
-    c_l.append(xchg(21, 1, lm.at[0], lgot.at[ts]))
+    c_l.append(xchg(23, 1, lm.at[0], lgot.at[ts]))
     lgot[ts] = lm[0]
     for cp in c_l:
         cp.wait_recv()
-    n = lax.broadcasted_iota(I32, (512, 256), 1)
-    r = lax.broadcasted_iota(I32, (512, 256), 0)
-    k = quarter_of(n)
-    goal = 128 * k + n - CQ * k
-    got = jnp.concatenate([lgot[i] for i in range(4)], 1)
-    for hh in range(2):
-        out[512 * hh : 512 * hh + 512, :] = dot(got, ones_at(r == goal + 64 * hh))[:, :172]
+    for k in range(4):
+        out[CQ * k : CQ * k + CQ, :] = lgot[k, 0:CQ, :].astype(F32)
 
     for t in range(4):
         drain1(t)
@@ -424,38 +486,34 @@
     features, self_weight1, neigh_weight1, need_first, count_first, adjacency_first,
     self_weight2, neigh_weight2, need_second, count_second, adjacency_second, seed_rows,
 ):
-    xs = features.reshape(128, 4, 4, 2, 32).transpose(1, 3, 0, 2, 4).reshape(4, 2, 8, 16, 128)
-    word = lax.broadcasted_iota(I32, (ROWS, WORDS), 1)
-    a1 = jnp.where(word < 8 * count_first[0], adjacency_first, 0).astype(BF)
-    a2 = jnp.where(word < 8 * count_second[0], adjacency_second, 0).astype(BF)
-    own_word = lax.broadcasted_iota(I32, (ROWS, 128), 1)
-    bit = jnp.left_shift(1, seed_rows % 16)
-    aq = jnp.where(own_word == (seed_rows // 16)[:, None], bit[:, None], 0).astype(BF)
-    needs = jnp.zeros((8, 128), I32).at[0, :64].set(need_first[0]).at[1, :64].set(need_second[0])
-
-    def classes(x):
-        return jnp.pad(x.reshape(128, 2, CQ), ((0, 0), (0, 0), (0, 64 - CQ))).reshape(128, 128)
-
-    w = jnp.concatenate(
-        [self_weight1, neigh_weight1, classes(self_weight2), classes(neigh_weight2)], 0
-    )
     vm = pl.BlockSpec(memory_space=pltpu.VMEM)
     sm = pl.BlockSpec(memory_space=pltpu.SMEM)
     dma = pltpu.SemaphoreType.DMA
-    return pl.pallas_call(
+    logits = pl.pallas_call(
         kernel,
-        out_shape=jax.ShapeDtypeStruct((ROWS, 172), F32),
-        in_specs=[sm] + [vm] * 6,
+        out_shape=jax.ShapeDtypeStruct((172, ROWS), F32),
+        in_specs=[sm] * 4 + [vm] * 8 + [pl.BlockSpec(memory_space=pl.ANY)] * 2,
         out_specs=vm,
         scratch_shapes=[
+            pltpu.VMEM((4, 2, 8, 16, 128), BF),
+            pltpu.VMEM((ROWS, WORDS), BF),
+            pltpu.VMEM((ROWS, WORDS), BF),
+            pltpu.VMEM((ROWS, 128), BF),
+            pltpu.VMEM((384, 128), BF),
+            pltpu.VMEM((ROWS, WORDS), I32),
+            pltpu.VMEM((ROWS, WORDS), I32),
+            pltpu.VMEM((2048, 128), F32),
+            pltpu.VMEM((128, 128), F32),
             *[pltpu.VMEM((256, 16, 128), BF)] * 4,
             *[pltpu.VMEM((256, 2, 16, 128), BF)] * 3,
             pltpu.VMEM((ROWS, WORDS), BF),
             pltpu.VMEM((ROWS, WORDS), BF),
             pltpu.VMEM((ROWS, 128), BF),
             pltpu.VMEM((4, 384, 128), BF),
-            pltpu.VMEM((8, 128), I32),
-            pltpu.SMEM((8, 128), I32),
+            pltpu.VMEM((1, 64), I32),
+            pltpu.VMEM((1, 64), I32),
+            pltpu.SMEM((1, 64), I32),
+            pltpu.SMEM((1, 64), I32),
             pltpu.VMEM((4, 8, 16, 128), BF),
             pltpu.VMEM((4, 128, 128), BF),
             pltpu.VMEM((4, 128, 128), BF),
@@ -464,25 +522,28 @@
             pltpu.VMEM((2 * ROWS, 256), F32),
             pltpu.VMEM((2 * ROWS, 128), F32),
             pltpu.VMEM((RB, 5 * WORDS), BF),
-            pltpu.VMEM((4 * WORDS, 128), BF),
-            pltpu.VMEM((5 * WORDS, 256), BF),
+            pltpu.VMEM((2, 4 * WORDS, 128), BF),
+            pltpu.VMEM((2, 5 * WORDS, 256), BF),
             pltpu.VMEM((2048, 128), BF),
-            pltpu.VMEM((WORDS, 128), BF),
-            pltpu.VMEM((2, WORDS, 128), BF),
             pltpu.VMEM((2, 512, 256), BF),
             pltpu.VMEM((4, 128, 256), BF),
             pltpu.VMEM((4, 4, 128, 128), BF),
             pltpu.VMEM((4, 4, 128, 128), BF),
-            pltpu.VMEM((2, 512, 128), BF),
-            pltpu.VMEM((4, 512, 128), BF),
+            pltpu.VMEM((2, 48, ROWS), BF),
+            pltpu.VMEM((4, 48, ROWS), BF),
             dma((4, 16)), dma((4,)), dma((4,)),
             dma((3, 16)), dma((3,)), dma((3,)),
-            dma((23,)), dma((23,)), dma(()),
+            dma((24,)), dma((24,)), dma((4,)),
         ],
         compiler_params=pltpu.CompilerParams(
             collective_id=0, has_side_effects=True, vmem_limit_bytes=60 * 2**20
         ),
-    )(needs, needs, xs, a1, a2, aq, w)
+    )(
+        need_first, need_second, count_first, count_second, need_first, need_second,
+        features.T, self_weight1, neigh_weight1, self_weight2.T, neigh_weight2.T,
+        seed_rows.reshape(8, 128), adjacency_first, adjacency_second,
+    )
+    return logits.T
 
 
 def solution(mesh):

time: 126 us -> 101 us (0.80)
  Pallas kernels: 109 us -> 96.4 us
  other arithmetic: 7.31 us -> 0 us
  local copies, waits for them, and re-layouts: 8.66 us -> 2.04 us
    pallas_call x1, Pallas kernels: 109 us -> 96.4 us  [per_device(): pl.pallas_call(kernel, out_shape=jax.ShapeDtypeStruct((172, ROWS), F32),...]
    convert_element_type x2 -> x0, other arithmetic: 5.18 us -> none  [the longest x1 4.14 us: per_device(): a2 = jnp.where(word < 8 * count_second[0], adjacency_second, 0).astype(BF)]
    reshape x6 -> x0, local copies, waits for them, and re-layouts: 3.34 us -> none  [the longest x2 1.62 us: per_device(): features.reshape(128, 4, 4, 2, 32).transpose(1, 3, 0, 2, 4)]
    pallas_call x1 -> x0, local copies, waits for them, and re-layouts: 2.4 us -> none  [per_device(): pl.pallas_call(kernel, out_shape=jax.ShapeDtypeStruct((ROWS, 172), F32),...]
    concatenate x1 -> x0, other arithmetic: 1.42 us -> none  [per_device(): jnp.concatenate([self_weight1, neigh_weight1, classes(self_weight2), clas...]
    scatter x2 -> x0, local copies, waits for them, and re-layouts: 1.41 us -> none  [per_device(): jnp.zeros((8, 128), I32).at[0, :64].set(need_first[0]).at[1, :64]]
where the time goes in v2:
time: 101 us; the launch traced here: 99.8 us
  Pallas kernels  96.4 us (95%)
  local copies, waits for them, and re-layouts  2.04 us (2%)
  between operations  1.31 us (1%)
    pallas_call x1, Pallas kernels, per_device(): pl.pallas_call(kernel, out_shape=jax.ShapeDtypeStruct((172, ROWS), F32),...  96.4 us
    unnamed x1, local copies, waits for them, and re-layouts  2.04 us

profile of v2, /device:TPU:0, one launch (start us, length us, event | category | flops | bytes accessed | tf_op | source)
XLA Modules:
  0.0 99.8 jit_solution(11181562534638797947)
XLA Ops:
  1.3 96.4 %shard_map.118 = f32[172,1024]{1,0:T(8,128)} custom-call(s32[1,64]{1,0:T(1,128)} %need1_v.1, s32[1,64]{1,0:T(1,128)} %need2_v.1, s32[1]{0:T(128)S(6)} %copy.14.count1, s32[1]{0:T(128)S(6)} %copy.15.count2, s32[1,64]{1,0:T(1,128)} %need1_v.1, s32[1,64]{1,0:T(1,128)} %need2_v.1, bf16[64,2048]{1,0:T(8,128)(2,1)} %bitcast.6, bf16[64,128]{1,0:T(8,128)(2,1)} %w1s.1, ...), custom_call_target="tpu_custom_call" | custom-call | tf_op jit(solution)/shard_map/pallas_call | solution.py:492
  97.7 2.0 %copy.16 = f32[1024,172]{0,1:T(8,128)} copy(f32[1024,172]{0,1:T(8,128)} %bitcast.5) | data formatting | bytes 1409024

commit v3 on v2

--- a/solution.py
+++ b/solution.py
@@ -232,7 +232,7 @@
     sx[pl.ds(2 * c, 2)] = xs[ts]
 
     rhs2[...] = jnp.zeros_like(rhs2)
-    run1("b0b1b2b3c0c1c2c3d0d1e0f0")
+    run1("b0b1b2b3c0c1c2c3d0d1e0d2e1f0")
     for cp in c_need:
         cp.wait_recv()
     to_smem = [
@@ -283,7 +283,7 @@
 
     loop(4, lambda k: pick1((0, 0), k))
     units = [(t, sl) for t in range(4) for sl in range(2)]
-    after = ["d2e1f1", "d3e2f2", "e3f3"] + [""] * 5
+    after = ["d3e2f1", "e3f2", "f3"] + [""] * 5
     for n, (t, sl) in enumerate(units):
         if n == 1:
             for cp in c_a1:
@@ -407,9 +407,30 @@
             return 0
 
         lax.fori_loop(0, ROWS // RB, own_rows, 0)
-        run2("c0c1" if s == 0 else "c2d0e0d1f0")
+        run2("c0c1" if s == 0 else "c2d0d1e0d2e1f0")
 
     m43 = lane_groups(5, CQ, 256)
+    l = lax.broadcasted_iota(I32, (48, 256), 1)
+    m = lax.broadcasted_iota(I32, (48, 256), 0)
+    fold = ones_at((m == l - CQ * quarter_of(l)) & (l < 5 * CQ))
+    fold_own = ones_at((m == (l & 63)) & (m < CQ))
+    fold = jnp.concatenate([fold, fold, fold_own], 1)
+
+    def split(x):
+        top = x.astype(BF)
+        return [top, (x - top.astype(F32)).astype(BF)]
+
+    def close(sl, i):
+        a = (a2, a2o)[sl][HB * i : HB * i + HB, :]
+        deg = dot(jnp.where(a != zero_bf, one_bf, zero_bf), ones)
+        deg = jnp.maximum(deg, 1.0)
+        at_rows = slice(sl * ROWS + HB * i, sl * ROWS + HB * i + HB)
+        x = acc2[at_rows, :] / jnp.concatenate([deg, deg], 1)
+        all_of = jnp.concatenate(split(x) + split(accq[at_rows, :]), 1)
+        lm[sl, :, HB * i : HB * i + HB] = lax.dot_general(
+            fold, all_of, (((1,), (1,)), ((), ())), preferred_element_type=F32
+        ).astype(BF)
+
     def pick2(unit, k):
         u, sl = unit
         for i in range(8):
@@ -422,7 +443,7 @@
 
     loop(4, lambda k: pick2((0, 0), k))
     units2 = [(u, sl) for u in range(3) for sl in range(2)]
-    after = ["d2e1f1", "", "e2f2"] + [""] * 3
+    after = ["e2f1", "", "f2"] + [""] * 3
     for n, (u, sl) in enumerate(units2):
 
         def rows2(i, n=n, u=u, sl=sl):
@@ -441,34 +462,17 @@
 
         loop(2, rows2)
         run2(after[n])
-
-    l = lax.broadcasted_iota(I32, (48, 256), 1)
-    m = lax.broadcasted_iota(I32, (48, 256), 0)
-    fold = ones_at((m == l - CQ * quarter_of(l)) & (l < 5 * CQ))
-    fold_own = ones_at((m == (l & 63)) & (m < CQ))
-    fold = jnp.concatenate([fold, fold, fold_own], 1)
-    c_l = []
-    for s in (1, 0):
-        adj = (a2, a2o)[s]
-
-        def split(x):
-            top = x.astype(BF)
-            return [top, (x - top.astype(F32)).astype(BF)]
-
-        for i in range(4):
-            a = adj[HB * i : HB * i + HB, :]
-            deg = dot(jnp.where(a != zero_bf, one_bf, zero_bf), ones)
-            deg = jnp.maximum(deg, 1.0)
-            at_rows = slice(s * ROWS + HB * i, s * ROWS + HB * i + HB)
-            x = acc2[at_rows, :] / jnp.concatenate([deg, deg], 1)
-            all_of = jnp.concatenate(split(x) + split(accq[at_rows, :]), 1)
-            lm[s, :, HB * i : HB * i + HB] = lax.dot_general(
-                fold, all_of, (((1,), (1,)), ((), ())), preferred_element_type=F32
-            ).astype(BF)
-        if s == 1:
-            c_l = [xchg(20, 0, lm.at[1], lgot.at[ts]), xchg(22, 2, lm.at[1], lgot.at[ts])]
-    c_l.append(xchg(23, 1, lm.at[0], lgot.at[ts]))
-    lgot[ts] = lm[0]
+        if n == 4:
+            for i in range(4):
+                close(0, i)
+            lgot[ts] = lm[0]
+            c_l = [xchg(23, 1, lm.at[0], lgot.at[ts])]
+    for hh in range(2):
+        close(1, 2 * hh)
+        close(1, 2 * hh + 1)
+        for e in (0, 2):
+            c_l.append(xchg(20 + 4 * hh + e, e, lm.at[1, :, h[hh]], lgot.at[ts, :, h[hh]]))
+
     for cp in c_l:
         cp.wait_recv()
     for k in range(4):
@@ -533,7 +537,7 @@
             pltpu.VMEM((4, 48, ROWS), BF),
             dma((4, 16)), dma((4,)), dma((4,)),
             dma((3, 16)), dma((3,)), dma((3,)),
-            dma((24,)), dma((24,)), dma((4,)),
+            dma((27,)), dma((27,)), dma((4,)),
         ],
         compiler_params=pltpu.CompilerParams(
             collective_id=0, has_side_effects=True, vmem_limit_bytes=60 * 2**20

time: 101 us -> 95.6 us (0.947)
  Pallas kernels: 96.4 us -> 91.4 us
    pallas_call x1, Pallas kernels: 96.4 us -> 91.4 us  [per_device(): pl.pallas_call(kernel, out_shape=jax.ShapeDtypeStruct((172, ROWS), F32),...]
where the time goes in v3:
time: 95.6 us; the launch traced here: 94.7 us
  Pallas kernels  91.4 us (96%)
  local copies, waits for them, and re-layouts  2.04 us (2%)
  between operations  1.31 us (1%)
    pallas_call x1, Pallas kernels, per_device(): pl.pallas_call(kernel, out_shape=jax.ShapeDtypeStruct((172, ROWS), F32),...  91.4 us
    unnamed x1, local copies, waits for them, and re-layouts  2.04 us

profile of v3, /device:TPU:0, one launch (start us, length us, event | category | flops | bytes accessed | tf_op | source)
XLA Modules:
  0.0 94.7 jit_solution(7432846940327523114)
XLA Ops:
  1.3 91.4 %shard_map.118 = f32[172,1024]{1,0:T(8,128)} custom-call(s32[1,64]{1,0:T(1,128)} %need1_v.1, s32[1,64]{1,0:T(1,128)} %need2_v.1, s32[1]{0:T(128)S(6)} %copy.14.count1, s32[1]{0:T(128)S(6)} %copy.15.count2, s32[1,64]{1,0:T(1,128)} %need1_v.1, s32[1,64]{1,0:T(1,128)} %need2_v.1, bf16[64,2048]{1,0:T(8,128)(2,1)} %bitcast.6, bf16[64,128]{1,0:T(8,128)(2,1)} %w1s.1, ...), custom_call_target="tpu_custom_call" | custom-call | tf_op jit(solution)/shard_map/pallas_call | solution.py:496
  92.7 2.0 %copy.16 = f32[1024,172]{0,1:T(8,128)} copy(f32[1024,172]{0,1:T(8,128)} %bitcast.5) | data formatting | bytes 1409024
